TPU v7x, 128 devices: a whole 4x4x4 slice. The times are simulated.
128 devices in a mesh: gz: 2 (over x_lo), gx: 2 (over core), gy: 32 (over z, y, x_hi).
Axes of the slice: x: 4 (x_hi: 2, x_lo: 2; x = x_hi * 2 + x_lo), y: 4, z: 4, core: 2. Of those that a mesh axis runs over, the one named last changes fastest.
Arguments:
- initial_field: float32 [128, 16, 4096], P('gz', 'gx', 'gy'), may hold values from -36 to 36
- plane_coupling: float32 [128, 16, 4096], P('gz', 'gx', 'gy'), may hold values from 0.06 to 0.24
- line_coupling: float32 [128, 16, 4096], P('gz', 'gx', 'gy'), may hold values from 1000 to 8000
- source: float32 [128, 16, 4096], P('gz', 'gx', 'gy'), may hold values from -4 to 4, as said below
- shift_table: float32 [8], replicated, may hold values from 0.5 to 1
- shift_index: int32 [4], replicated, may hold values from 0 to 7
Outputs:
- heated: float32 [128, 16, 4096], P('gz', 'gx', 'gy')
Inputs may be any that keep to these rules, and one draw needn't show every extreme that they name: `shift_index`: one table row for each half-step. A heat source.
All inputs are finite; a program needn't handle non-finite values.
Results may differ from a plain program's by a relative error of at most 0.0003.
Values sent between devices are 32-bit elements; how exact they have to be, the bound alone decides.
A program may use at most 64 MiB of HBM per device.

v0:
```python
import functools

import jax
import jax.numpy as jnp
from jax import lax
from jax.experimental import pallas as pl
from jax.experimental.pallas import tpu as pltpu
from jax.sharding import PartitionSpec as P


EXPLICIT = 32
SUMS = 8
PACK = 16
UNPACK = 16
FACTOR = 8


def loop(count, body, init, unroll, reverse=False):
    while count % unroll:
        unroll -= 1

    def block(i, carry):
        for j in range(unroll):
            k = i * unroll + j
            carry = body(count - 1 - k if reverse else k, carry)
        return carry

    return lax.fori_loop(0, count // unroll, block, init)


def kernel(
    ny_parts, half,
    u_in, pc_in, lc_in, src_in, table, index,
    out,
    u_x, pc_x, lc_x, src_x, to_left, to_right, from_left, from_right,
    p_s, own_s, near_s, src_s, b_s, g_s, f_s, w_s, iq_s, beta_s, beta_r, face_s, face_r,
    in_sem, xs_sem, xr_sem, ys_sem, yr_sem, bs_sem, br_sem, fs_sem, fr_sem,
):
    n, rows, lanes = u_in.shape
    width = half
    per = lanes // width
    groups = n // per
    gz, gx, gy = lax.axis_index("gz"), lax.axis_index("gx"), lax.axis_index("gy")
    has_left, has_right = gy > 0, gy < ny_parts - 1
    own_r, own_c = pl.ds(0, rows), pl.ds(0, lanes)
    other_r, halo_c = pl.ds(rows, rows), pl.ds(lanes, lanes)
    all_r = pl.ds(0, 2 * rows)
    ins = (u_in, pc_in, lc_in, src_in)
    exts = (u_x, pc_x, lc_x, src_x)

    loads = [
        pltpu.make_async_copy(i, e.at[:, own_r, own_c], in_sem.at[a])
        for a, (i, e) in enumerate(zip(ins, exts))
    ]
    for c in loads:
        c.start()

    barrier = pltpu.get_barrier_semaphore()

    def greet(device):
        pl.semaphore_signal(
            barrier, inc=1, device_id=device, device_id_type=pl.DeviceIdType.MESH
        )

    x_peer = (gz, 1 - gx, gy)
    z_peer = (1 - gz, gx, gy)
    left = ((gz, gx, gy - 1), (gz, 1 - gx, gy - 1))
    right = ((gz, gx, gy + 1), (gz, 1 - gx, gy + 1))
    greet(x_peer)
    greet(z_peer)

    @pl.when(has_left)
    def _():
        greet(left[0])
        greet(left[1])

    @pl.when(has_right)
    def _():
        greet(right[0])
        greet(right[1])

    for c in loads:
        c.wait()

    lane = lax.broadcasted_iota(jnp.int32, (rows, lanes), 1)

    def slot(j):
        return (lane >= j * width) & (lane < j * width + width)

    def pack(j, carry):
        at_right = slot(j)
        at_left = slot(lax.rem(j + 1, per))
        done = []
        for i, (e, g) in enumerate((e, g) for e in exts for g in range(groups)):
            t = pltpu.roll(e[g * per + j, own_r, own_c], (lax.rem(j + 1, per)) * width, 1)
            r, l = carry[i]
            done.append((jnp.where(at_right, t, r), jnp.where(at_left, t, l)))
        return tuple(done)

    zero = jnp.zeros((rows, lanes), jnp.float32)
    packed = loop(per, pack, tuple((zero, zero) for _ in range(4 * groups)), PACK)
    for i, (r, l) in enumerate(packed):
        to_right[i] = r
        to_left[i] = l

    lefts_there = (gy + ny_parts - 1) // ny_parts
    rights_there = (2 * ny_parts - 2 - gy) // ny_parts
    pl.semaphore_wait(barrier, 2 + 2 * lefts_there + 2 * rights_there)

    def remote(src, dst, send, recv, device):
        return pltpu.make_async_remote_copy(
            src_ref=src, dst_ref=dst, send_sem=send, recv_sem=recv,
            device_id=device, device_id_type=pl.DeviceIdType.MESH,
        )

    lefts = [
        remote(to_left, from_right.at[t], ys_sem.at[t], yr_sem.at[t], left[t]) for t in range(2)
    ]
    rights = [
        remote(to_right, from_left.at[t], ys_sem.at[2 + t], yr_sem.at[2 + t], right[t])
        for t in range(2)
    ]

    @pl.when(has_left)
    def _():
        for c in lefts:
            c.start()

    @pl.when(has_right)
    def _():
        for c in rights:
            c.start()

    xs = [
        remote(
            e.at[:, own_r, own_c], e.at[:, other_r, own_c], xs_sem.at[a], xr_sem.at[a], x_peer
        )
        for a, e in enumerate(exts)
    ]
    for a in (2, 0, 1, 3):
        xs[a].start()

    def layer(k):
        return k + gz * (n - 1 - 2 * k)

    def shift(h):
        return table[index[h]]

    def inverse(h, shape):
        return 1.0 / jnp.full(shape, shift(h), jnp.float32)

    def factor(r_at, c_at, hs):
        shape = (r_at.size, lanes)
        inv = inverse_all(hs, shape)
        one = jnp.ones(shape, jnp.float32)

        def body(k, carry):
            z = layer(k)
            rl = 1.0 / lc_x[z, r_at, c_at]
            pc, src = pc_x[z, r_at, c_at], src_x[z, r_at, c_at]
            four = 4.0 * pc
            done = []
            for (p, d), h, i in zip(carry, hs, inv):
                d = d + (rl * i) * p
                q = p + d
                p_s[h, z, r_at, c_at] = p
                pr = p * rl
                own_s[h, z, r_at, c_at] = pr * (i - four)
                near_s[h, z, r_at, c_at] = pr * pc
                src_s[h, z, r_at, c_at] = pr * src
                b_s[h, z, r_at, c_at] = 1.0 / (p * q)
                done.append((q, d))
            return tuple(done)

        final = loop(n, body, tuple((one, one) for _ in hs), FACTOR)
        for (q, d), h in zip(final, hs):
            iq = 1.0 / q
            iq_s[h, r_at, c_at] = iq
            beta_s[h, r_at, c_at] = d * iq

    def inverse_all(hs, shape):
        return [inverse(h, shape) for h in hs]

    steps = list(range(half))
    factor(own_r, own_c, steps)
    for a in (2, 0, 1, 3):
        xs[a].wait()
    factor(other_r, own_c, steps[:-1])

    def send_beta(h, c_at, i):
        return remote(
            beta_s.at[h, :, c_at], beta_r.at[h, :, c_at], bs_sem.at[i], br_sem.at[i], z_peer
        )

    last = half - 1
    betas = [[send_beta(h, own_c, h)] for h in steps[:-1]]
    betas.append(
        [remote(
            beta_s.at[last, own_r, own_c], beta_r.at[last, own_r, own_c],
            bs_sem.at[last], br_sem.at[last], z_peer,
        )]
    )
    for b in betas:
        b[0].start()

    @pl.when(has_left)
    def _():
        for c in lefts:
            c.wait_send()
        for c in rights:
            c.wait_recv()

    @pl.when(has_right)
    def _():
        for c in rights:
            c.wait_send()
        for c in lefts:
            c.wait_recv()

    inside = ((lane < width) & has_right) | ((lane >= lanes - width) & has_left)

    filler = lc_x[0, own_r, own_c]

    def unpack(j, carry):
        at_left = slot(lax.rem(j + 1, per))
        back = (per - 1 - j) * width
        for t in range(2):
            r_at = pl.ds(t * rows, rows)
            for a, e in enumerate(exts):
                for g in range(groups):
                    i = a * groups + g
                    both = jnp.where(at_left, from_right[t, i], from_left[t, i])
                    z = g * per + j
                    rest = filler if a == 2 else zero
                    e[z, r_at, halo_c] = jnp.where(inside, pltpu.roll(both, back, 1), rest)
        return carry

    loop(per, unpack, 0, UNPACK)

    def factor_halo(h):
        factor(all_r, halo_c, [h])
        c = send_beta(h, halo_c, half + h)
        c.start()
        betas[h].append(c)

    factor_halo(0)

    wide = (2 * rows, 2 * lanes)
    row = lax.broadcasted_iota(jnp.int32, wide, 0)
    top = row == gx * rows
    bottom = row == (2 * rows - 1 + gx * rows) % (2 * rows)

    def edges(u):
        return (
            jnp.where(top, 0.0, pltpu.roll(u, 1, 0))
            + jnp.where(bottom, 0.0, pltpu.roll(u, 2 * rows - 1, 0))
            + pltpu.roll(u, 1, 1)
            + pltpu.roll(u, 2 * lanes - 1, 1)
        )

    def explicit(h, field):
        r_at, c_at, shape, cut = part(h)

        def body(k, total):
            z = layer(k)
            u = field(z)
            beside = cut(edges(u))
            g = own_s[h, z, r_at, c_at] * cut(u) + (
                near_s[h, z, r_at, c_at] * beside + src_s[h, z, r_at, c_at]
            )
            g_s[z, r_at, c_at] = g
            return total + g

        return loop(n, body, jnp.zeros(shape, jnp.float32), EXPLICIT)

    def part(h):
        if h == last:
            return own_r, own_c, (rows, lanes), lambda a: a[:rows, :lanes]
        return all_r, pl.ds(0, 2 * lanes), wide, lambda a: a

    total = explicit(0, lambda z: u_x[z])
    for h in steps:
        r_at, c_at, shape, _ = part(h)
        iq = iq_s[h, r_at, c_at]
        face = total * iq
        face_s[h, r_at, c_at] = face
        send = remote(
            face_s.at[h, r_at, c_at], face_r.at[h, r_at, c_at], fs_sem.at[h], fr_sem.at[h], z_peer
        )
        send.start()
        zero_part = jnp.zeros(shape, jnp.float32)

        def ahead(k, total, h=h, r_at=r_at, c_at=c_at):
            z = layer(k)
            total = total + g_s[z, r_at, c_at]
            f_s[z, r_at, c_at] = total * b_s[h, z, r_at, c_at]
            return total

        def behind(k, total, h=h, r_at=r_at, c_at=c_at):
            z = layer(k)
            total = total + f_s[z, r_at, c_at]
            w_s[z, r_at, c_at] = p_s[h, z, r_at, c_at] * total
            return total

        loop(n, ahead, zero_part, SUMS)
        loop(n, behind, zero_part, SUMS, reverse=True)
        if h + 1 < last:
            factor_halo(h + 1)
        for b in betas[h]:
            b.wait()
        mine, theirs = beta_s[h, r_at, c_at], beta_r[h, r_at, c_at]
        gain = iq / (mine + theirs - mine * theirs)
        partial = (1.0 - theirs) * face
        send.wait()
        v = (face_r[h, r_at, c_at] + partial) * gain

        def solved(z, h=h, v=v, r_at=r_at, c_at=c_at):
            return p_s[h, z, r_at, c_at] * v + w_s[z, r_at, c_at]

        if h < last:
            total = explicit(h + 1, solved)
        else:

            def write(z, carry):
                out[z] = solved(z)
                return carry

            loop(n, write, 0, SUMS)


def solution(mesh):
    ny_parts = mesh.shape["gy"]
    assert mesh.shape["gz"] == 2 and mesh.shape["gx"] == 2

    def on_device(u, pc, lc, src, table, index):
        half = index.shape[0]
        n, rows, lanes = u.shape
        f32 = jnp.float32
        ext = pltpu.VMEM((n, 2 * rows, 2 * lanes), f32)
        coef = pltpu.VMEM((half, n, 2 * rows, 2 * lanes), f32)
        face = pltpu.VMEM((half, 2 * rows, 2 * lanes), f32)
        count = 4 * (n * half // lanes)
        pack = pltpu.VMEM((count, rows, lanes), f32)
        packs = pltpu.VMEM((2, count, rows, lanes), f32)
        dma = pltpu.SemaphoreType.DMA
        return pl.pallas_call(
            functools.partial(kernel, ny_parts, half),
            out_shape=pltpu.VMEM(u.shape, f32),
            in_specs=[pl.BlockSpec(memory_space=pl.ANY)] * 4
            + [pl.BlockSpec(memory_space=pltpu.SMEM)] * 2,
            out_specs=pl.BlockSpec(memory_space=pltpu.VMEM),
            scratch_shapes=[ext] * 4 + [pack] * 2 + [packs] * 2
            + [coef] * 5 + [ext] * 3 + [face] * 5
            + [dma((4,)), dma((4,)), dma((4,)), dma((4,)), dma((4,)),
               dma((2 * half,)), dma((2 * half,)), dma((half,)), dma((half,))],
            compiler_params=pltpu.CompilerParams(collective_id=0, has_side_effects=True),
        )(u, pc, lc, src, table, index)

    spec = P("gz", "gx", "gy")
    return jax.shard_map(
        on_device, mesh=mesh, in_specs=(spec,) * 4 + (P(), P()), out_specs=spec, check_vma=False
    )
```

profile of v0, /device:TPU:96, one launch (start us, length us, event | category | flops | bytes accessed | tf_op | source)
XLA Modules:
  0.0 26.4 jit_solution(5087508526876817223)
XLA Ops:
  0.0 25.6 %shard_map.64 = f32[64,8,128]{2,1,0:T(8,128)S(1)} custom-call(f32[64,8,128]{2,1,0:T(8,128)} %u_in.1, f32[64,8,128]{2,1,0:T(8,128)} %pc_in.1, f32[64,8,128]{2,1,0:T(8,128)} %lc_in.1, f32[64,8,128]{2,1,0:T(8,128)} %src_in.1, f32[8]{0:T(128)} %table.1, s32[4]{0:T(128)} %index.1), custom_call_target="tpu_custom_call" | custom-call | tf_op jit(solution)/shard_map/pallas_call | solution.py:346
  25.7 0.7 %copy.8 = f32[64,8,128]{2,1,0:T(8,128)} copy(f32[64,8,128]{2,1,0:T(8,128)S(1)} %shard_map.64) | data formatting | bytes 524288
where the time goes:
time: 26.5 us; the launch traced here: 26.4 us
  Pallas kernels  25.6 us (97%)
  local copies, waits for them, and re-layouts  0.71 us (3%)
    pallas_call x1, Pallas kernels, on_device(): pl.pallas_call(functools.partial(kernel, ny_parts, half), out_shape=pltpu...  25.6 us
    unnamed x1, local copies, waits for them, and re-layouts  0.71 us

commit v1 on v0

v1 whole, which is shorter than its diff:
```python
import functools

import jax
import jax.numpy as jnp
from jax import lax
from jax.experimental import pallas as pl
from jax.experimental.pallas import tpu as pltpu
from jax.sharding import PartitionSpec as P


CORE = 1
EDGE_AT = 2
EXPLICIT = 16
BEHIND = 32
FACTOR = 8
SLOTS = 16
WIDTH = 8


def loop(count, body, init, unroll, reverse=False):
    while count % unroll:
        unroll -= 1

    def block(i, carry):
        for j in range(unroll):
            k = i * unroll + j
            carry = body(count - 1 - k if reverse else k, carry)
        return carry

    return lax.fori_loop(0, count // unroll, block, init)


def tree(items, slot):
    bit = 0
    while len(items) > 1:
        odd = (slot >> bit) & 1 == 1
        items = [jnp.where(odd, b, a) for a, b in zip(items[::2], items[1::2])]
        bit += 1
    return items[0]


def kernel(
    ny_parts, half,
    u_in, pc_in, lc_in, src_in, table, index,
    out,
    u_x, pc_x, lc_x, src_x, rl_s, p_s, b_s, f_s, t_s,
    un_s, tr_s, pr_s, un_r, tr_r, pr_r, beta_s, beta_r, iq_s, iq_r, face_s, face_r,
    pk, yk, eo, en, eu, epc, elc, esrc, erl, ep, eb, ef, ret_s, ret_r,
    in_sem, un_sem, tr_ss, tr_rs, pr_ss, pr_rs, be_ss, be_rs, iq_ss, iq_rs, fa_ss, fa_rs,
    y_ss, y_rs, e_ss, e_rs, ret_ss, ret_rs,
):
    n, rows, lanes = u_in.shape
    last = half - 1
    groups = n // SLOTS
    gz, gx, gy = lax.axis_index("gz"), lax.axis_index("gx"), lax.axis_index("gy")
    has_left, has_right = gy > 0, gy < ny_parts - 1
    owner = gx == CORE
    lefts_there = (gy + ny_parts - 1) // ny_parts
    rights_there = (2 * ny_parts - 2 - gy) // ny_parts
    there = (lefts_there, rights_there)
    sides = (lax.rem(gy + ny_parts - 1, ny_parts), lax.rem(gy + 1, ny_parts))
    at_z, at_x = (1 - gz, gz), (1 - gx, gx)
    has_side = at_z[0] * lefts_there + at_z[1] * rights_there == 1
    me = 2 * gz + gx
    full = (rows, lanes)

    loads = [
        pltpu.make_async_copy(i, x, in_sem.at[a])
        for a, (i, x) in enumerate(((u_in, u_x), (pc_in, pc_x), (lc_in, lc_x), (src_in, src_x)))
    ]
    for a in (2, 0, 1, 3):
        loads[a].start()

    barrier = pltpu.get_barrier_semaphore()

    def greet(device):
        pl.semaphore_signal(
            barrier, inc=1, device_id=device, device_id_type=pl.DeviceIdType.MESH
        )

    def when_side(act):
        for s in range(2):

            @pl.when(at_x[CORE] * at_z[s] * there[s] == 1)
            def _(s=s):
                act(sides[s])

    def greet_side(side):
        for q in range(4):
            greet((q // 2, q % 2, side))

    when_side(greet_side)

    z_peer, x_peer, d_peer = (1 - gz, gx, gy), (gz, 1 - gx, gy), (1 - gz, 1 - gx, gy)
    peers = (z_peer, x_peer, d_peer)
    for peer in peers:
        greet(peer)

    def remote(src, dst, send, recv, device):
        return pltpu.make_async_remote_copy(
            src_ref=src, dst_ref=dst, send_sem=send, recv_sem=recv,
            device_id=device, device_id_type=pl.DeviceIdType.MESH,
        )

    def layer(k):
        return k + gz * (n - 1 - 2 * k)

    def shift(h):
        return table[index[h]]

    def inverse(h):
        return 1.0 / jnp.full(full, shift(h), jnp.float32)

    lane = lax.broadcasted_iota(jnp.int32, full, 1)
    row = lax.broadcasted_iota(jnp.int32, full, 0)

    is_low = gx == 0

    def edge(x):
        return jnp.where(is_low, x[rows - 1:rows], x[0:1])

    def factor(coupling, p_ref, b_ref, rl_ref, hs, make, row_ref=None):
        inv = [inverse(h) for h in hs]
        one = jnp.ones(full, jnp.float32)

        def body(k, carry):
            if make:
                rl = 1.0 / coupling(k)
                rl_ref[k] = rl
            else:
                rl = rl_ref[k]
            done = []
            for (p, d), h, i in zip(carry, hs, inv):
                d = d + (rl * i) * p
                q = p + d
                p_ref[h, k] = p
                if row_ref is not None and h < last:
                    row_ref[h, k] = edge(p)
                b_ref[h, k] = 1.0 / (p * q)
                done.append((q, d))
            return tuple(done)

        final = loop(n, body, tuple((one, one) for _ in hs), FACTOR)
        ends = []
        for q, d in final:
            iq = 1.0 / q
            ends.append((iq, d * iq))
        return ends

    def meet(face, beta, iq, face_n, beta_n):
        gain = iq / (beta + beta_n - beta * beta_n)
        return (face_n + (1.0 - beta_n) * face) * gain

    loads[2].wait()
    ends = factor(lambda k: lc_x[layer(k)], p_s, b_s, rl_s, [0], True, pr_s)
    iqs = [e[0] for e in ends]
    iq_s[0] = ends[0][0]
    beta_s[0] = ends[0][1]

    for a in (0, 1, 3):
        loads[a].wait()

    base = 64 * gz + 16 * gx
    low = lane % WIDTH < WIDTH // 2
    fields = (u_x, pc_x, lc_x, src_x)

    def pack(pair, carry):
        for a, e in enumerate(fields):
            packed = []
            for s in range(2):
                g = 2 * pair + s
                moved = []
                for j in range(SLOTS):
                    x = e[layer(g * SLOTS + j)]
                    if a == 0:
                        un_s[g * SLOTS + j] = edge(x)
                    moved.append(pltpu.roll(x, (4 + 8 * j + 4 * s) % lanes, 1))
                at_left = ((lane - 4 - 4 * s) & (lanes - 1)) // WIDTH
                at_right = ((lane + 4 - 4 * s) & (lanes - 1)) // WIDTH
                l = pltpu.roll(tree(moved, at_left), base, 1)
                r = pltpu.roll(tree(moved, at_right), base, 1)
                pk[0, a * groups + g] = l
                pk[1, a * groups + g] = r
                packed.append((l, r))
            (l0, r0), (l1, r1) = packed
            yk[0, a * (groups // 2) + pair] = jnp.where(low, l1, l0)
            yk[1, a * (groups // 2) + pair] = jnp.where(low, r0, r1)
        return carry

    lax.fori_loop(0, groups // 2, pack, 0)

    pl.semaphore_wait(barrier, 3 + lefts_there + rights_there)

    def to_left(q):
        return remote(yk.at[0], en.at[q], y_ss.at[0], y_rs.at[q], (1, CORE, sides[0]))

    def to_right(q):
        return remote(yk.at[1], en.at[q], y_ss.at[1], y_rs.at[q], (0, CORE, sides[1]))

    for q in range(4):

        here = at_z[q // 2] * at_x[q % 2]

        @pl.when(here * lefts_there == 1)
        def _(q=q):
            to_left(q).start()

        @pl.when(here * rights_there == 1)
        def _(q=q):
            to_right(q).start()

    un = remote(un_s, un_r, un_sem.at[0], un_sem.at[1], x_peer)
    un.start()

    def send_betas(h):
        for s, peer in enumerate(peers):
            if s == 0 or h < last:
                c = remote(beta_s.at[h], beta_r.at[h, s], be_ss.at[3 * h + s], be_rs.at[3 * h + s], peer)
                c.start()
                betas[h].append(c)
        if h < last:
            c = remote(iq_s.at[h], iq_r.at[h], iq_ss.at[h], iq_rs.at[h], x_peer)
            c.start()
            betas[h].append(c)
            c = remote(pr_s.at[h], pr_r.at[h], pr_ss.at[h], pr_rs.at[h], x_peer)
            c.start()
            betas[h].append(c)

    betas = [[] for _ in range(half)]
    send_betas(0)

    def to_owner(s, q):
        return remote(pk.at[s], eo.at[q], e_ss.at[s], e_rs.at[q], (s, CORE, gy))

    for q in range(4):
        for s in range(2):
            if q != 2 * s + CORE:

                @pl.when(me == q)
                def _(s=s, q=q):
                    to_owner(s, q).start()

    top_in, bottom_in = gx == 1, gx == 0

    def beside_own(u, other):
        up = jnp.where(row == 0, jnp.where(top_in, other, 0.0), pltpu.roll(u, 1, 0))
        down = jnp.where(
            row == rows - 1, jnp.where(bottom_in, other, 0.0), pltpu.roll(u, rows - 1, 0)
        )
        return (up + down) + (pltpu.roll(u, 1, 1) + pltpu.roll(u, lanes - 1, 1))

    def spread(r):
        return jnp.broadcast_to(r, full)

    def explicit_own(h, v, vn):
        inv = inverse(h)

        def body(k, total):
            z = layer(k)
            if h == 0:
                u, other = u_x[z], spread(un_r[k])
            else:
                u = p_s[h - 1, k] * (v + t_s[k])
                other = spread(pr_r[h - 1, k]) * (vn + spread(tr_r[h - 1, k]))
            e = inv * u + pc_x[z] * (beside_own(u, other) - 4.0 * u) + src_x[z]
            total = total + (p_s[h, k] * rl_s[k]) * e
            f_s[k] = total * b_s[h, k]
            return total

        return loop(n, body, jnp.zeros(full, jnp.float32), EXPLICIT)

    def behind_own(send):
        def body(k, total):
            total = total + f_s[k]
            t_s[k] = total
            if send:
                tr_s[k] = edge(total)
            return total

        loop(n, body, jnp.zeros(full, jnp.float32), BEHIND, reverse=True)

    shifted = lane + 4 * gz

    def edge_wait():
        def waiting(slot, ref, sems):
            remote(ref.at[slot], ref.at[slot], e_ss.at[0], sems.at[slot], x_peer).wait_recv()

        def wait_side(side):
            for slot in range(4):
                waiting(slot, en, y_rs)

        for s in range(2):

            @pl.when(at_x[CORE] * at_z[s] == 1)
            def _(s=s):
                for i in range(4 * groups):
                    eo[2 * s + CORE, i] = pk[s, i]
                for slot in range(4):
                    if slot != 2 * s + CORE:
                        waiting(slot, eo, e_rs)

        when_side(wait_side)

    def edge_unpack():

        filler = lc_x[0]
        zero = jnp.zeros(full, jnp.float32)
        targets = (eu, epc, elc, esrc)

        def unpack(pair, carry):
            for a, e in enumerate(targets):
                rest = filler if a == 2 else zero
                near = [
                    jnp.where(has_side, en[q, a * (groups // 2) + pair], rest) for q in range(4)
                ]
                for s in range(2):
                    g = 2 * pair + s
                    mine = [eo[q, a * groups + g] for q in range(4)]
                    both = {}
                    for m in range(4):
                        x = (shifted - 8 * m - 4 * s) & (lanes - 1)
                        rg = (x // 16) & 1 == 1
                        rel = x & 15
                        from_near = jnp.where(
                            gz == 0, (rel < 4).astype(jnp.int32),
                            ((rel >= 8) & (rel < 12)).astype(jnp.int32),
                        ) == 1
                        for zh in range(2):
                            o = jnp.where(rg, mine[2 * zh + 1], mine[2 * zh])
                            w = jnp.where(rg, near[2 * zh + 1], near[2 * zh])
                            both[m, zh] = jnp.where(from_near, w, o)
                    for j in range(SLOTS):
                        x = (shifted - 8 * j - 4 * s) & (lanes - 1)
                        v = jnp.where(x >= 64, both[j % 4, 1], both[j % 4, 0])
                        e[g * SLOTS + j] = pltpu.roll(v, (lanes - 8 * j - 4 * s) % lanes, 1)
            return carry

        lax.fori_loop(0, groups // 2, unpack, 0)

    def edges():
        edge_unpack()
        ends = factor(lambda k: elc[k], ep, eb, erl, list(range(half)), True)
        in_second = (shifted // 16) & 1 == 1
        top, bottom = row == 0, row == rows - 1
        for h in range(half):
            inv = inverse(h)

            def explicit(k, total, h=h, inv=inv):
                u = eu[k]
                up, down = pltpu.roll(u, 1, 0), pltpu.roll(u, rows - 1, 0)
                up = jnp.where(
                    top, jnp.where(in_second, pltpu.roll(up, 16, 1), 0.0), up
                )
                down = jnp.where(
                    bottom, jnp.where(in_second, 0.0, pltpu.roll(down, lanes - 16, 1)), down
                )
                beside = (up + down) + (pltpu.roll(u, 1, 1) + pltpu.roll(u, lanes - 1, 1))
                e = inv * u + epc[k] * (beside - 4.0 * u) + esrc[k]
                total = total + (ep[h, k] * erl[k]) * e
                ef[k] = total * eb[h, k]
                return total

            total = loop(n, explicit, jnp.zeros(full, jnp.float32), EXPLICIT)
            iq, beta = ends[h]
            face = total * iq
            v = meet(face, beta, iq, pltpu.roll(face, 64, 1), pltpu.roll(beta, 64, 1))

            def behind(k, total, h=h):
                total = total + ef[k]
                eu[k] = ep[h, k] * total
                return total

            loop(n, behind, v, BEHIND, reverse=True)

        def give(g, carry):
            moved = [pltpu.roll(eu[g * SLOTS + j], 8 * j, 1) for j in range(SLOTS)]
            for q in range(4):
                at = (lane // WIDTH - 8 * (q // 2) - 2 * (q % 2)) & (SLOTS - 1)
                b = 64 * (q // 2) + 16 * (q % 2)
                ret_s[q, g] = pltpu.roll(tree(moved, at), (lanes - b) % lanes, 1)
            return carry

        lax.fori_loop(0, groups, give, 0)
        for s in range(2):

            @pl.when(gz == s)
            def _(s=s):
                for q in range(4):
                    if q != 2 * s + CORE:
                        remote(
                            ret_s.at[q], ret_r.at[s], ret_ss.at[q], ret_rs.at[s],
                            (q // 2, q % 2, gy),
                        ).start()
                for g in range(groups):
                    ret_r[s, g] = ret_s[2 * s + CORE, g]

    un.wait()
    v = vn = None
    faces = []
    tails = []
    for h in range(half):
        total = explicit_own(h, v, vn)
        face = total * iq_s[h]
        face_s[h] = face
        sends = []
        for s, peer in enumerate(peers):
            if s == 0 or h < last:
                c = remote(face_s.at[h], face_r.at[h, s], fa_ss.at[3 * h + s], fa_rs.at[3 * h + s], peer)
                c.start()
                sends.append(c)
        faces.append(sends)
        if h == 0:
            hs = list(range(1, half))
            for i, (iq, beta) in zip(hs, factor(None, p_s, b_s, rl_s, hs, False, pr_s)):
                iq_s[i] = iq
                beta_s[i] = beta
        behind_own(h < last)
        if h < last:
            c = remote(tr_s, tr_r.at[h], tr_ss.at[h], tr_rs.at[h], x_peer)
            c.start()
            tails.append(c)
        if h == 0:
            for i in hs:
                send_betas(i)
        if h == EDGE_AT:

            edge_wait()

            @pl.when(owner)
            def _():
                edges()

        for c in betas[h]:
            c.wait()
        if h < last:
            tails[h].wait()
        for c in sends:
            c.wait()
        iq, beta = iq_s[h], beta_s[h]
        v = meet(face_s[h], beta, iq, face_r[h, 0], beta_r[h, 0])
        if h < last:
            w = meet(face_r[h, 1], beta_r[h, 1], iq_r[h], face_r[h, 2], beta_r[h, 2])
            vn = jnp.where(is_low, spread(w[0:1]), spread(w[rows - 1:rows]))

    for s in range(2):

        @pl.when(me != 2 * s + CORE)
        def _(s=s):
            remote(
                ret_s.at[0], ret_r.at[s], ret_ss.at[0], ret_rs.at[s], x_peer
            ).wait_recv()

    outer = (lane < 4) | (lane >= lanes - 4)

    def write(g, carry):
        both = jnp.where(low, ret_r[1, g], ret_r[0, g])
        for j in range(SLOTS):
            k = g * SLOTS + j
            u = p_s[last, k] * (v + t_s[k])
            out[layer(k)] = jnp.where(outer, pltpu.roll(both, (lanes - 4 - 8 * j) % lanes, 1), u)
        return carry

    lax.fori_loop(0, groups, write, 0)

    @pl.when(has_left)
    def _():
        to_left(0).wait_send()

    @pl.when(has_right)
    def _():
        to_right(0).wait_send()

    for s in range(2):

        @pl.when(me != 2 * s + CORE)
        def _(s=s):
            to_owner(s, 0).wait_send()

    @pl.when(owner)
    def _():
        for q in range(4):

            @pl.when(me != q)
            def _(q=q):
                remote(
                    ret_s.at[q], ret_r.at[0], ret_ss.at[q], ret_rs.at[0], x_peer
                ).wait_send()


def solution(mesh):
    ny_parts = mesh.shape["gy"]
    assert mesh.shape["gz"] == 2 and mesh.shape["gx"] == 2

    def on_device(u, pc, lc, src, table, index):
        half = index.shape[0]
        n, rows, lanes = u.shape
        groups = n // SLOTS
        assert (rows, lanes, half) == (8, 128, 4) and n % (2 * SLOTS) == 0

        def vmem(*dims):
            return pltpu.VMEM(dims, jnp.float32)

        def tiles(*dims):
            return vmem(*dims, rows, lanes)

        dma = pltpu.SemaphoreType.DMA
        scratch = [tiles(n)] * 5 + [tiles(half, n)] * 2 + [tiles(n)] * 2
        scratch += [vmem(n, 1, lanes), vmem(n, 1, lanes), vmem(half - 1, n, 1, lanes)]
        scratch += [vmem(n, 1, lanes), vmem(half - 1, n, 1, lanes), vmem(half - 1, n, 1, lanes)]
        scratch += [tiles(half), tiles(half, 3), tiles(half), tiles(half - 1)]
        scratch += [tiles(half), tiles(half, 3)]
        scratch += [tiles(2, 4 * groups), tiles(2, 2 * groups), tiles(4, 4 * groups), tiles(4, 2 * groups)]
        scratch += [tiles(n)] * 5 + [tiles(half, n)] * 2 + [tiles(n)]
        scratch += [tiles(4, groups), tiles(2, groups)]
        scratch += [dma((4,)), dma((2,))]
        scratch += [dma((half - 1,))] * 4
        scratch += [dma((3 * half,))] * 2
        scratch += [dma((half - 1,))] * 2
        scratch += [dma((3 * half,))] * 2
        scratch += [dma((2,)), dma((4,)), dma((2,)), dma((4,)), dma((4,)), dma((2,))]
        return pl.pallas_call(
            functools.partial(kernel, ny_parts, half),
            out_shape=pltpu.VMEM(u.shape, jnp.float32),
            in_specs=[pl.BlockSpec(memory_space=pl.ANY)] * 4
            + [pl.BlockSpec(memory_space=pltpu.SMEM)] * 2,
            out_specs=pl.BlockSpec(memory_space=pltpu.VMEM),
            scratch_shapes=scratch,
            compiler_params=pltpu.CompilerParams(collective_id=0, has_side_effects=True),
        )(u, pc, lc, src, table, index)

    spec = P("gz", "gx", "gy")
    return jax.shard_map(
        on_device, mesh=mesh, in_specs=(spec,) * 4 + (P(), P()), out_specs=spec, check_vma=False
    )
```

time: 26.5 us -> 22.4 us (0.85)
  the two profiles are of different devices: /device:TPU:96 before, /device:TPU:97 now
where the time goes in v1:
time: 22.4 us; the launch traced here: 22.3 us
  Pallas kernels  21.5 us (96%)
  local copies, waits for them, and re-layouts  0.71 us (3%)
    pallas_call x1, Pallas kernels, on_device(): pl.pallas_call(functools.partial(kernel, ny_parts, half), out_shape=pltpu...  21.5 us
    unnamed x1, local copies, waits for them, and re-layouts  0.71 us

profile of v1, /device:TPU:97, one launch (start us, length us, event | category | flops | bytes accessed | tf_op | source)
XLA Modules:
  0.0 22.3 jit_solution(727624574232769607)
XLA Ops:
  0.0 21.5 %shard_map.64 = f32[64,8,128]{2,1,0:T(8,128)S(1)} custom-call(f32[64,8,128]{2,1,0:T(8,128)} %u_in.1, f32[64,8,128]{2,1,0:T(8,128)} %pc_in.1, f32[64,8,128]{2,1,0:T(8,128)} %lc_in.1, f32[64,8,128]{2,1,0:T(8,128)} %src_in.1, f32[8]{0:T(128)} %table.1, s32[4]{0:T(128)} %index.1), custom_call_target="tpu_custom_call" | custom-call | tf_op jit(solution)/shard_map/pallas_call | solution.py:521
  21.6 0.7 %copy.8 = f32[64,8,128]{2,1,0:T(8,128)} copy(f32[64,8,128]{2,1,0:T(8,128)S(1)} %shard_map.64) | data formatting | bytes 524288

commit v2 on v1

--- a/solution.py
+++ b/solution.py
@@ -47,7 +47,7 @@
     un_s, tr_s, pr_s, un_r, tr_r, pr_r, beta_s, beta_r, iq_s, iq_r, face_s, face_r,
     pk, yk, eo, en, eu, epc, elc, esrc, erl, ep, eb, ef, ret_s, ret_r,
     in_sem, un_sem, tr_ss, tr_rs, pr_ss, pr_rs, be_ss, be_rs, iq_ss, iq_rs, fa_ss, fa_rs,
-    y_ss, y_rs, e_ss, e_rs, ret_ss, ret_rs,
+    group_sem, far_sem, y_ss, y_rs, e_ss, e_rs, ret_ss, ret_rs,
 ):
     n, rows, lanes = u_in.shape
     last = half - 1
@@ -78,23 +78,19 @@
             barrier, inc=1, device_id=device, device_id_type=pl.DeviceIdType.MESH
         )
 
-    def when_side(act):
-        for s in range(2):
-
-            @pl.when(at_x[CORE] * at_z[s] * there[s] == 1)
-            def _(s=s):
-                act(sides[s])
-
-    def greet_side(side):
-        for q in range(4):
-            greet((q // 2, q % 2, side))
-
-    when_side(greet_side)
-
     z_peer, x_peer, d_peer = (1 - gz, gx, gy), (gz, 1 - gx, gy), (1 - gz, 1 - gx, gy)
     peers = (z_peer, x_peer, d_peer)
     for peer in peers:
         greet(peer)
+
+    def when_side(act):
+        for s in range(2):
+
+            @pl.when(at_x[CORE] * at_z[s] * there[s] == 1)
+            def _(s=s):
+                act(s)
+
+    when_side(lambda s: greet((1 - s, CORE, sides[s])))
 
     def remote(src, dst, send, recv, device):
         return pltpu.make_async_remote_copy(
@@ -189,25 +185,20 @@
 
     lax.fori_loop(0, groups // 2, pack, 0)
 
-    pl.semaphore_wait(barrier, 3 + lefts_there + rights_there)
-
-    def to_left(q):
-        return remote(yk.at[0], en.at[q], y_ss.at[0], y_rs.at[q], (1, CORE, sides[0]))
-
-    def to_right(q):
-        return remote(yk.at[1], en.at[q], y_ss.at[1], y_rs.at[q], (0, CORE, sides[1]))
-
-    for q in range(4):
-
-        here = at_z[q // 2] * at_x[q % 2]
-
-        @pl.when(here * lefts_there == 1)
-        def _(q=q):
-            to_left(q).start()
-
-        @pl.when(here * rights_there == 1)
-        def _(q=q):
-            to_right(q).start()
+    def tell(sem, device):
+        pl.semaphore_signal(sem, inc=1, device_id=device, device_id_type=pl.DeviceIdType.MESH)
+
+    @pl.when(gx != CORE)
+    def _():
+        pl.semaphore_wait(barrier, 3)
+        tell(group_sem, x_peer)
+
+    @pl.when(gx == CORE)
+    def _():
+        pl.semaphore_wait(group_sem, 1)
+
+    def to_side(s, q):
+        return remote(yk.at[s], en.at[q], y_ss.at[s], y_rs.at[q], (1 - s, CORE, sides[s]))
 
     un = remote(un_s, un_r, un_sem.at[0], un_sem.at[1], x_peer)
     un.start()
@@ -285,7 +276,7 @@
         def waiting(slot, ref, sems):
             remote(ref.at[slot], ref.at[slot], e_ss.at[0], sems.at[slot], x_peer).wait_recv()
 
-        def wait_side(side):
+        def wait_side(s):
             for slot in range(4):
                 waiting(slot, en, y_rs)
 
@@ -300,6 +291,26 @@
                         waiting(slot, eo, e_rs)
 
         when_side(wait_side)
+
+    def far_sends():
+        @pl.when(gx == CORE)
+        def _():
+            pl.semaphore_wait(barrier, 3 + at_z[0] * lefts_there + at_z[1] * rights_there)
+
+        def relay(s):
+            for peer in peers:
+                tell(far_sem.at[s], peer)
+
+        when_side(relay)
+        for q in range(4):
+            for s in range(2):
+                here = at_z[q // 2] * at_x[q % 2] * there[s]
+
+                @pl.when(here == 1)
+                def _(q=q, s=s):
+                    if q != 2 * s + CORE:
+                        pl.semaphore_wait(far_sem.at[s], 1)
+                    to_side(s, q).start()
 
     def edge_unpack():
 
@@ -410,6 +421,8 @@
                 sends.append(c)
         faces.append(sends)
         if h == 0:
+            far_sends()
+        if h == 0:
             hs = list(range(1, half))
             for i, (iq, beta) in zip(hs, factor(None, p_s, b_s, rl_s, hs, False, pr_s)):
                 iq_s[i] = iq
@@ -464,11 +477,11 @@
 
     @pl.when(has_left)
     def _():
-        to_left(0).wait_send()
+        to_side(0, 0).wait_send()
 
     @pl.when(has_right)
     def _():
-        to_right(0).wait_send()
+        to_side(1, 0).wait_send()
 
     for s in range(2):
 
@@ -517,6 +530,7 @@
         scratch += [dma((3 * half,))] * 2
         scratch += [dma((half - 1,))] * 2
         scratch += [dma((3 * half,))] * 2
+        scratch += [pltpu.SemaphoreType.REGULAR, pltpu.SemaphoreType.REGULAR((2,))]
         scratch += [dma((2,)), dma((4,)), dma((2,)), dma((4,)), dma((4,)), dma((2,))]
         return pl.pallas_call(
             functools.partial(kernel, ny_parts, half),

time: 22.4 us -> 21 us (0.938)
  the two profiles are of different devices: /device:TPU:97 before, /device:TPU:1 now
where the time goes in v2:
time: 21 us; the launch traced here: 20.9 us
  Pallas kernels  20.2 us (96%)
  local copies, waits for them, and re-layouts  0.71 us (3%)
    pallas_call x1, Pallas kernels, on_device(): pl.pallas_call(functools.partial(kernel, ny_parts, half), out_shape=pltpu...  20.2 us
    unnamed x1, local copies, waits for them, and re-layouts  0.71 us

profile of v2, /device:TPU:1, one launch (start us, length us, event | category | flops | bytes accessed | tf_op | source)
XLA Modules:
  0.0 20.9 jit_solution(6083364913311799509)
XLA Ops:
  0.0 20.2 %shard_map.64 = f32[64,8,128]{2,1,0:T(8,128)S(1)} custom-call(f32[64,8,128]{2,1,0:T(8,128)} %u_in.1, f32[64,8,128]{2,1,0:T(8,128)} %pc_in.1, f32[64,8,128]{2,1,0:T(8,128)} %lc_in.1, f32[64,8,128]{2,1,0:T(8,128)} %src_in.1, f32[8]{0:T(128)} %table.1, s32[4]{0:T(128)} %index.1), custom_call_target="tpu_custom_call" | custom-call | tf_op jit(solution)/shard_map/pallas_call | solution.py:535
  20.2 0.7 %copy.8 = f32[64,8,128]{2,1,0:T(8,128)} copy(f32[64,8,128]{2,1,0:T(8,128)S(1)} %shard_map.64) | data formatting | bytes 524288

commit v3 on v2

--- a/solution.py
+++ b/solution.py
@@ -10,8 +10,10 @@
 
 CORE = 1
 EDGE_AT = 2
-EXPLICIT = 16
-BEHIND = 32
+EDGE_SPLIT = 4
+EXPLICIT = 64
+BEHIND = 64
+CHUNK = 8
 FACTOR = 8
 SLOTS = 16
 WIDTH = 8
@@ -45,7 +47,7 @@
     out,
     u_x, pc_x, lc_x, src_x, rl_s, p_s, b_s, f_s, t_s,
     un_s, tr_s, pr_s, un_r, tr_r, pr_r, beta_s, beta_r, iq_s, iq_r, face_s, face_r,
-    pk, yk, eo, en, eu, epc, elc, esrc, erl, ep, eb, ef, ret_s, ret_r,
+    pk, yk, eo, en, eu, epc, elc, esrc, erl, ep, eb, ef, eiq, ebeta, ret_s, ret_r,
     in_sem, un_sem, tr_ss, tr_rs, pr_ss, pr_rs, be_ss, be_rs, iq_ss, iq_rs, fa_ss, fa_rs,
     group_sem, far_sem, y_ss, y_rs, e_ss, e_rs, ret_ss, ret_rs,
 ):
@@ -60,7 +62,8 @@
     there = (lefts_there, rights_there)
     sides = (lax.rem(gy + ny_parts - 1, ny_parts), lax.rem(gy + 1, ny_parts))
     at_z, at_x = (1 - gz, gz), (1 - gx, gx)
-    has_side = at_z[0] * lefts_there + at_z[1] * rights_there == 1
+    side = 1 - gz
+    has_side = at_z[1] * lefts_there + at_z[0] * rights_there == 1
     me = 2 * gz + gx
     full = (rows, lanes)
 
@@ -86,11 +89,11 @@
     def when_side(act):
         for s in range(2):
 
-            @pl.when(at_x[CORE] * at_z[s] * there[s] == 1)
+            @pl.when(at_x[CORE] * at_z[1 - s] * there[s] == 1)
             def _(s=s):
                 act(s)
 
-    when_side(lambda s: greet((1 - s, CORE, sides[s])))
+    when_side(lambda s: greet((s, CORE, sides[s])))
 
     def remote(src, dst, send, recv, device):
         return pltpu.make_async_remote_copy(
@@ -127,8 +130,9 @@
                 rl = rl_ref[k]
             done = []
             for (p, d), h, i in zip(carry, hs, inv):
-                d = d + (rl * i) * p
-                q = p + d
+                add = (rl * i) * p
+                q = (p + d) + add
+                d = d + add
                 p_ref[h, k] = p
                 if row_ref is not None and h < last:
                     row_ref[h, k] = edge(p)
@@ -156,7 +160,7 @@
     for a in (0, 1, 3):
         loads[a].wait()
 
-    base = 64 * gz + 16 * gx
+    base = 16 * gz + 64 * gx
     low = lane % WIDTH < WIDTH // 2
     fields = (u_x, pc_x, lc_x, src_x)
 
@@ -198,7 +202,7 @@
         pl.semaphore_wait(group_sem, 1)
 
     def to_side(s, q):
-        return remote(yk.at[s], en.at[q], y_ss.at[s], y_rs.at[q], (1 - s, CORE, sides[s]))
+        return remote(yk.at[s], en.at[q], y_ss.at[s], y_rs.at[q], (s, CORE, sides[s]))
 
     un = remote(un_s, un_r, un_sem.at[0], un_sem.at[1], x_peer)
     un.start()
@@ -221,11 +225,11 @@
     send_betas(0)
 
     def to_owner(s, q):
-        return remote(pk.at[s], eo.at[q], e_ss.at[s], e_rs.at[q], (s, CORE, gy))
+        return remote(pk.at[s], eo.at[q], e_ss.at[s], e_rs.at[q], (1 - s, CORE, gy))
 
     for q in range(4):
         for s in range(2):
-            if q != 2 * s + CORE:
+            if q != 2 * (1 - s) + CORE:
 
                 @pl.when(me == q)
                 def _(s=s, q=q):
@@ -260,17 +264,29 @@
 
         return loop(n, body, jnp.zeros(full, jnp.float32), EXPLICIT)
 
+    def suffix(terms, init, put):
+        def block(i, total):
+            for c in range(BEHIND // CHUNK):
+                first = n - CHUNK * (c + 1) - i * BEHIND
+                parts = [terms[first + CHUNK - 1]]
+                for j in range(1, CHUNK):
+                    parts.append(parts[-1] + terms[first + CHUNK - 1 - j])
+                for j, part in enumerate(parts):
+                    put(first + CHUNK - 1 - j, total + part)
+                total = total + parts[-1]
+            return total
+
+        lax.fori_loop(0, n // BEHIND, block, init)
+
     def behind_own(send):
-        def body(k, total):
-            total = total + f_s[k]
+        def put(k, total):
             t_s[k] = total
             if send:
                 tr_s[k] = edge(total)
-            return total
-
-        loop(n, body, jnp.zeros(full, jnp.float32), BEHIND, reverse=True)
-
-    shifted = lane + 4 * gz
+
+        suffix(f_s, jnp.zeros(full, jnp.float32), put)
+
+    shifted = lane + 4 * side
 
     def edge_wait():
         def waiting(slot, ref, sems):
@@ -282,12 +298,12 @@
 
         for s in range(2):
 
-            @pl.when(at_x[CORE] * at_z[s] == 1)
+            @pl.when(at_x[CORE] * at_z[1 - s] == 1)
             def _(s=s):
                 for i in range(4 * groups):
-                    eo[2 * s + CORE, i] = pk[s, i]
+                    eo[2 * (1 - s) + CORE, i] = pk[s, i]
                 for slot in range(4):
-                    if slot != 2 * s + CORE:
+                    if slot != 2 * (1 - s) + CORE:
                         waiting(slot, eo, e_rs)
 
         when_side(wait_side)
@@ -295,7 +311,7 @@
     def far_sends():
         @pl.when(gx == CORE)
         def _():
-            pl.semaphore_wait(barrier, 3 + at_z[0] * lefts_there + at_z[1] * rights_there)
+            pl.semaphore_wait(barrier, 3 + at_z[1] * lefts_there + at_z[0] * rights_there)
 
         def relay(s):
             for peer in peers:
@@ -308,7 +324,7 @@
 
                 @pl.when(here == 1)
                 def _(q=q, s=s):
-                    if q != 2 * s + CORE:
+                    if q != 2 * (1 - s) + CORE:
                         pl.semaphore_wait(far_sem.at[s], 1)
                     to_side(s, q).start()
 
@@ -330,16 +346,16 @@
                     both = {}
                     for m in range(4):
                         x = (shifted - 8 * m - 4 * s) & (lanes - 1)
-                        rg = (x // 16) & 1 == 1
+                        odd = (x // 16) & 1 == 1
                         rel = x & 15
                         from_near = jnp.where(
-                            gz == 0, (rel < 4).astype(jnp.int32),
+                            side == 0, (rel < 4).astype(jnp.int32),
                             ((rel >= 8) & (rel < 12)).astype(jnp.int32),
                         ) == 1
-                        for zh in range(2):
-                            o = jnp.where(rg, mine[2 * zh + 1], mine[2 * zh])
-                            w = jnp.where(rg, near[2 * zh + 1], near[2 * zh])
-                            both[m, zh] = jnp.where(from_near, w, o)
+                        for rg in range(2):
+                            o = jnp.where(odd, mine[2 + rg], mine[rg])
+                            w = jnp.where(odd, near[2 + rg], near[rg])
+                            both[m, rg] = jnp.where(from_near, w, o)
                     for j in range(SLOTS):
                         x = (shifted - 8 * j - 4 * s) & (lanes - 1)
                         v = jnp.where(x >= 64, both[j % 4, 1], both[j % 4, 0])
@@ -348,62 +364,67 @@
 
         lax.fori_loop(0, groups // 2, unpack, 0)
 
-    def edges():
-        edge_unpack()
+    x_at = shifted & (lanes - 1)
+    far_rows, far_layers = x_at >= 64, (x_at // 16) & 1 == 1
+    top, bottom = row == 0, row == rows - 1
+    across = (top & far_rows) | (bottom & ~far_rows)
+
+    def other_half(a):
+        return jnp.where(far_layers, pltpu.roll(a, 16, 1), pltpu.roll(a, lanes - 16, 1))
+
+    def edge_factor():
         ends = factor(lambda k: elc[k], ep, eb, erl, list(range(half)), True)
-        in_second = (shifted // 16) & 1 == 1
-        top, bottom = row == 0, row == rows - 1
-        for h in range(half):
-            inv = inverse(h)
-
-            def explicit(k, total, h=h, inv=inv):
-                u = eu[k]
-                up, down = pltpu.roll(u, 1, 0), pltpu.roll(u, rows - 1, 0)
-                up = jnp.where(
-                    top, jnp.where(in_second, pltpu.roll(up, 16, 1), 0.0), up
-                )
-                down = jnp.where(
-                    bottom, jnp.where(in_second, 0.0, pltpu.roll(down, lanes - 16, 1)), down
-                )
-                beside = (up + down) + (pltpu.roll(u, 1, 1) + pltpu.roll(u, lanes - 1, 1))
-                e = inv * u + epc[k] * (beside - 4.0 * u) + esrc[k]
-                total = total + (ep[h, k] * erl[k]) * e
-                ef[k] = total * eb[h, k]
-                return total
-
-            total = loop(n, explicit, jnp.zeros(full, jnp.float32), EXPLICIT)
-            iq, beta = ends[h]
-            face = total * iq
-            v = meet(face, beta, iq, pltpu.roll(face, 64, 1), pltpu.roll(beta, 64, 1))
-
-            def behind(k, total, h=h):
-                total = total + ef[k]
-                eu[k] = ep[h, k] * total
-                return total
-
-            loop(n, behind, v, BEHIND, reverse=True)
-
+        for h, (iq, beta) in enumerate(ends):
+            eiq[h] = iq
+            ebeta[h] = beta
+
+    def edge_step(h):
+        inv = inverse(h)
+
+        def explicit(k, total):
+            u = eu[k]
+            up, down = pltpu.roll(u, 1, 0), pltpu.roll(u, rows - 1, 0)
+            over = pltpu.roll(jnp.where(top, up, down), 64, 1)
+            over = jnp.where(across, over, 0.0)
+            up, down = jnp.where(top, over, up), jnp.where(bottom, over, down)
+            beside = (up + down) + (pltpu.roll(u, 1, 1) + pltpu.roll(u, lanes - 1, 1))
+            e = inv * u + epc[k] * (beside - 4.0 * u) + esrc[k]
+            total = total + (ep[h, k] * erl[k]) * e
+            ef[k] = total * eb[h, k]
+            return total
+
+        total = loop(n, explicit, jnp.zeros(full, jnp.float32), EXPLICIT)
+        iq, beta = eiq[h], ebeta[h]
+        face = total * iq
+        v = meet(face, beta, iq, other_half(face), other_half(beta))
+
+        def put(k, total):
+            eu[k] = ep[h, k] * total
+
+        suffix(ef, v, put)
+
+    def edge_give():
         def give(g, carry):
             moved = [pltpu.roll(eu[g * SLOTS + j], 8 * j, 1) for j in range(SLOTS)]
             for q in range(4):
-                at = (lane // WIDTH - 8 * (q // 2) - 2 * (q % 2)) & (SLOTS - 1)
-                b = 64 * (q // 2) + 16 * (q % 2)
+                b = 16 * (q // 2) + 64 * (q % 2)
+                at = ((lane - b) & (lanes - 1)) // WIDTH
                 ret_s[q, g] = pltpu.roll(tree(moved, at), (lanes - b) % lanes, 1)
             return carry
 
         lax.fori_loop(0, groups, give, 0)
         for s in range(2):
 
-            @pl.when(gz == s)
+            @pl.when(gz == 1 - s)
             def _(s=s):
                 for q in range(4):
-                    if q != 2 * s + CORE:
+                    if q != 2 * (1 - s) + CORE:
                         remote(
                             ret_s.at[q], ret_r.at[s], ret_ss.at[q], ret_rs.at[s],
                             (q // 2, q % 2, gy),
                         ).start()
                 for g in range(groups):
-                    ret_r[s, g] = ret_s[2 * s + CORE, g]
+                    ret_r[s, g] = ret_s[2 * (1 - s) + CORE, g]
 
     un.wait()
     v = vn = None
@@ -436,12 +457,22 @@
             for i in hs:
                 send_betas(i)
         if h == EDGE_AT:
-
             edge_wait()
 
             @pl.when(owner)
             def _():
-                edges()
+                edge_unpack()
+                edge_factor()
+                for i in range(EDGE_SPLIT):
+                    edge_step(i)
+
+        if h == EDGE_AT:
+
+            @pl.when(owner)
+            def _():
+                for i in range(EDGE_SPLIT, half):
+                    edge_step(i)
+                edge_give()
 
         for c in betas[h]:
             c.wait()
@@ -457,7 +488,7 @@
 
     for s in range(2):
 
-        @pl.when(me != 2 * s + CORE)
+        @pl.when(me != 2 * (1 - s) + CORE)
         def _(s=s):
             remote(
                 ret_s.at[0], ret_r.at[s], ret_ss.at[0], ret_rs.at[s], x_peer
@@ -485,7 +516,7 @@
 
     for s in range(2):
 
-        @pl.when(me != 2 * s + CORE)
+        @pl.when(me != 2 * (1 - s) + CORE)
         def _(s=s):
             to_owner(s, 0).wait_send()
 
@@ -523,7 +554,7 @@
         scratch += [tiles(half), tiles(half, 3), tiles(half), tiles(half - 1)]
         scratch += [tiles(half), tiles(half, 3)]
         scratch += [tiles(2, 4 * groups), tiles(2, 2 * groups), tiles(4, 4 * groups), tiles(4, 2 * groups)]
-        scratch += [tiles(n)] * 5 + [tiles(half, n)] * 2 + [tiles(n)]
+        scratch += [tiles(n)] * 5 + [tiles(half, n)] * 2 + [tiles(n)] + [tiles(half)] * 2
         scratch += [tiles(4, groups), tiles(2, groups)]
         scratch += [dma((4,)), dma((2,))]
         scratch += [dma((half - 1,))] * 4

time: 21 us -> 18.9 us (0.90)
  the two profiles are of different devices: /device:TPU:1 before, /device:TPU:97 now
where the time goes in v3:
time: 18.9 us; the launch traced here: 18.8 us
  Pallas kernels  18.1 us (96%)
  local copies, waits for them, and re-layouts  0.71 us (4%)
    pallas_call x1, Pallas kernels, on_device(): pl.pallas_call(functools.partial(kernel, ny_parts, half), out_shape=pltpu...  18.1 us
    unnamed x1, local copies, waits for them, and re-layouts  0.71 us

profile of v3, /device:TPU:97, one launch (start us, length us, event | category | flops | bytes accessed | tf_op | source)
XLA Modules:
  0.0 18.8 jit_solution(6993697811357857756)
XLA Ops:
  0.0 18.1 %shard_map.64 = f32[64,8,128]{2,1,0:T(8,128)S(1)} custom-call(f32[64,8,128]{2,1,0:T(8,128)} %u_in.1, f32[64,8,128]{2,1,0:T(8,128)} %pc_in.1, f32[64,8,128]{2,1,0:T(8,128)} %lc_in.1, f32[64,8,128]{2,1,0:T(8,128)} %src_in.1, f32[8]{0:T(128)} %table.1, s32[4]{0:T(128)} %index.1), custom_call_target="tpu_custom_call" | custom-call | tf_op jit(solution)/shard_map/pallas_call | solution.py:566
  18.1 0.7 %copy.8 = f32[64,8,128]{2,1,0:T(8,128)} copy(f32[64,8,128]{2,1,0:T(8,128)S(1)} %shard_map.64) | data formatting | bytes 524288

commit v4 on v3

--- a/solution.py
+++ b/solution.py
@@ -14,7 +14,7 @@
 EXPLICIT = 64
 BEHIND = 64
 CHUNK = 8
-FACTOR = 8
+FACTOR = 64
 SLOTS = 16
 WIDTH = 8
 
@@ -93,7 +93,11 @@
             def _(s=s):
                 act(s)
 
-    when_side(lambda s: greet((s, CORE, sides[s])))
+    def greet_far(s):
+        for z in range(2):
+            greet((z, CORE, sides[s]))
+
+    when_side(greet_far)
 
     def remote(src, dst, send, recv, device):
         return pltpu.make_async_remote_copy(
@@ -187,7 +191,8 @@
             yk[1, a * (groups // 2) + pair] = jnp.where(low, r0, r1)
         return carry
 
-    lax.fori_loop(0, groups // 2, pack, 0)
+    for i in range(groups // 2):
+        pack(i, 0)
 
     def tell(sem, device):
         pl.semaphore_signal(sem, inc=1, device_id=device, device_id_type=pl.DeviceIdType.MESH)
@@ -311,21 +316,19 @@
     def far_sends():
         @pl.when(gx == CORE)
         def _():
-            pl.semaphore_wait(barrier, 3 + at_z[1] * lefts_there + at_z[0] * rights_there)
-
-        def relay(s):
-            for peer in peers:
-                tell(far_sem.at[s], peer)
-
-        when_side(relay)
+            pl.semaphore_wait(barrier, 3 + lefts_there + rights_there)
+            tell(far_sem, x_peer)
+
+        @pl.when(gx != CORE)
+        def _():
+            pl.semaphore_wait(far_sem, 1)
+
         for q in range(4):
             for s in range(2):
                 here = at_z[q // 2] * at_x[q % 2] * there[s]
 
                 @pl.when(here == 1)
                 def _(q=q, s=s):
-                    if q != 2 * (1 - s) + CORE:
-                        pl.semaphore_wait(far_sem.at[s], 1)
                     to_side(s, q).start()
 
     def edge_unpack():
@@ -362,7 +365,8 @@
                         e[g * SLOTS + j] = pltpu.roll(v, (lanes - 8 * j - 4 * s) % lanes, 1)
             return carry
 
-        lax.fori_loop(0, groups // 2, unpack, 0)
+        for i in range(groups // 2):
+            unpack(i, 0)
 
     x_at = shifted & (lanes - 1)
     far_rows, far_layers = x_at >= 64, (x_at // 16) & 1 == 1
@@ -412,7 +416,8 @@
                 ret_s[q, g] = pltpu.roll(tree(moved, at), (lanes - b) % lanes, 1)
             return carry
 
-        lax.fori_loop(0, groups, give, 0)
+        for i in range(groups):
+            give(i, 0)
         for s in range(2):
 
             @pl.when(gz == 1 - s)
@@ -504,7 +509,8 @@
             out[layer(k)] = jnp.where(outer, pltpu.roll(both, (lanes - 4 - 8 * j) % lanes, 1), u)
         return carry
 
-    lax.fori_loop(0, groups, write, 0)
+    for i in range(groups):
+        write(i, 0)
 
     @pl.when(has_left)
     def _():
@@ -561,7 +567,7 @@
         scratch += [dma((3 * half,))] * 2
         scratch += [dma((half - 1,))] * 2
         scratch += [dma((3 * half,))] * 2
-        scratch += [pltpu.SemaphoreType.REGULAR, pltpu.SemaphoreType.REGULAR((2,))]
+        scratch += [pltpu.SemaphoreType.REGULAR] * 2
         scratch += [dma((2,)), dma((4,)), dma((2,)), dma((4,)), dma((4,)), dma((2,))]
         return pl.pallas_call(
             functools.partial(kernel, ny_parts, half),

time: 18.9 us -> 17.9 us (0.947)
  Pallas kernels: 18.1 us -> 16.9 us
    pallas_call x1, Pallas kernels: 18.1 us -> 16.9 us  [on_device(): pl.pallas_call(functools.partial(kernel, ny_parts, half), out_shape=pltpu...]
where the time goes in v4:
time: 17.9 us; the launch traced here: 17.7 us
  Pallas kernels  16.9 us (94%)
  local copies, waits for them, and re-layouts  0.71 us (4%)
    pallas_call x1, Pallas kernels, on_device(): pl.pallas_call(functools.partial(kernel, ny_parts, half), out_shape=pltpu...  16.9 us
    unnamed x1, local copies, waits for them, and re-layouts  0.71 us

profile of v4, /device:TPU:97, one launch (start us, length us, event | category | flops | bytes accessed | tf_op | source)
XLA Modules:
  0.0 17.7 jit_solution(4934727419399634413)
XLA Ops:
  0.0 16.9 %shard_map.64 = f32[64,8,128]{2,1,0:T(8,128)S(1)} custom-call(f32[64,8,128]{2,1,0:T(8,128)} %u_in.1, f32[64,8,128]{2,1,0:T(8,128)} %pc_in.1, f32[64,8,128]{2,1,0:T(8,128)} %lc_in.1, f32[64,8,128]{2,1,0:T(8,128)} %src_in.1, f32[8]{0:T(128)} %table.1, s32[4]{0:T(128)} %index.1), custom_call_target="tpu_custom_call" | custom-call | tf_op jit(solution)/shard_map/pallas_call | solution.py:572
  17.0 0.7 %copy.8 = f32[64,8,128]{2,1,0:T(8,128)} copy(f32[64,8,128]{2,1,0:T(8,128)S(1)} %shard_map.64) | data formatting | bytes 524288

commit v5 on v4

--- a/solution.py
+++ b/solution.py
@@ -161,8 +161,9 @@
     iq_s[0] = ends[0][0]
     beta_s[0] = ends[0][1]
 
-    for a in (0, 1, 3):
-        loads[a].wait()
+    loads[0].wait()
+    for k in range(n):
+        un_s[k] = edge(u_x[layer(k)])
 
     base = 16 * gz + 64 * gx
     low = lane % WIDTH < WIDTH // 2
@@ -176,8 +177,6 @@
                 moved = []
                 for j in range(SLOTS):
                     x = e[layer(g * SLOTS + j)]
-                    if a == 0:
-                        un_s[g * SLOTS + j] = edge(x)
                     moved.append(pltpu.roll(x, (4 + 8 * j + 4 * s) % lanes, 1))
                 at_left = ((lane - 4 - 4 * s) & (lanes - 1)) // WIDTH
                 at_right = ((lane + 4 - 4 * s) & (lanes - 1)) // WIDTH
@@ -191,8 +190,6 @@
             yk[1, a * (groups // 2) + pair] = jnp.where(low, r0, r1)
         return carry
 
-    for i in range(groups // 2):
-        pack(i, 0)
 
     def tell(sem, device):
         pl.semaphore_signal(sem, inc=1, device_id=device, device_id_type=pl.DeviceIdType.MESH)
@@ -232,14 +229,6 @@
     def to_owner(s, q):
         return remote(pk.at[s], eo.at[q], e_ss.at[s], e_rs.at[q], (1 - s, CORE, gy))
 
-    for q in range(4):
-        for s in range(2):
-            if q != 2 * (1 - s) + CORE:
-
-                @pl.when(me == q)
-                def _(s=s, q=q):
-                    to_owner(s, q).start()
-
     top_in, bottom_in = gx == 1, gx == 0
 
     def beside_own(u, other):
@@ -312,6 +301,15 @@
                         waiting(slot, eo, e_rs)
 
         when_side(wait_side)
+
+    def own_sends():
+        for q in range(4):
+            for s in range(2):
+                if q != 2 * (1 - s) + CORE:
+
+                    @pl.when(me == q)
+                    def _(s=s, q=q):
+                        to_owner(s, q).start()
 
     def far_sends():
         @pl.when(gx == CORE)
@@ -431,6 +429,10 @@
                 for g in range(groups):
                     ret_r[s, g] = ret_s[2 * (1 - s) + CORE, g]
 
+    for a in (1, 3):
+        loads[a].wait()
+    for i in range(groups // 2):
+        pack(i, 0)
     un.wait()
     v = vn = None
     faces = []
@@ -448,6 +450,7 @@
         faces.append(sends)
         if h == 0:
             far_sends()
+            own_sends()
         if h == 0:
             hs = list(range(1, half))
             for i, (iq, beta) in zip(hs, factor(None, p_s, b_s, rl_s, hs, False, pr_s)):

time: 17.9 us -> 17.2 us (0.961)
  the two profiles are of different devices: /device:TPU:97 before, /device:TPU:98 now
where the time goes in v5:
time: 17.2 us; the launch traced here: 17 us
  Pallas kernels  16.3 us (95%)
  local copies, waits for them, and re-layouts  0.71 us (4%)
    pallas_call x1, Pallas kernels, on_device(): pl.pallas_call(functools.partial(kernel, ny_parts, half), out_shape=pltpu...  16.3 us
    unnamed x1, local copies, waits for them, and re-layouts  0.71 us

profile of v5, /device:TPU:98, one launch (start us, length us, event | category | flops | bytes accessed | tf_op | source)
XLA Modules:
  0.0 17.0 jit_solution(18210819967726831863)
XLA Ops:
  0.0 16.3 %shard_map.64 = f32[64,8,128]{2,1,0:T(8,128)S(1)} custom-call(f32[64,8,128]{2,1,0:T(8,128)} %u_in.1, f32[64,8,128]{2,1,0:T(8,128)} %pc_in.1, f32[64,8,128]{2,1,0:T(8,128)} %lc_in.1, f32[64,8,128]{2,1,0:T(8,128)} %src_in.1, f32[8]{0:T(128)} %table.1, s32[4]{0:T(128)} %index.1), custom_call_target="tpu_custom_call" | custom-call | tf_op jit(solution)/shard_map/pallas_call | solution.py:575
  16.3 0.7 %copy.8 = f32[64,8,128]{2,1,0:T(8,128)} copy(f32[64,8,128]{2,1,0:T(8,128)S(1)} %shard_map.64) | data formatting | bytes 524288

commit v6 on v5

--- a/solution.py
+++ b/solution.py
@@ -231,12 +231,14 @@
 
     top_in, bottom_in = gx == 1, gx == 0
 
+    shared = row == (rows - 1) * gx
+    border = row == (rows - 1) * (1 - gx)
+    towards = 1 + (rows - 2) * (1 - gx)
+
     def beside_own(u, other):
-        up = jnp.where(row == 0, jnp.where(top_in, other, 0.0), pltpu.roll(u, 1, 0))
-        down = jnp.where(
-            row == rows - 1, jnp.where(bottom_in, other, 0.0), pltpu.roll(u, rows - 1, 0)
-        )
-        return (up + down) + (pltpu.roll(u, 1, 1) + pltpu.roll(u, lanes - 1, 1))
+        inner = pltpu.roll(jnp.where(shared, other, u), towards, 0)
+        outer = pltpu.roll(jnp.where(border, 0.0, u), rows - towards, 0)
+        return (inner + outer) + (pltpu.roll(u, 1, 1) + pltpu.roll(u, lanes - 1, 1))
 
     def spread(r):
         return jnp.broadcast_to(r, full)
@@ -451,17 +453,16 @@
         if h == 0:
             far_sends()
             own_sends()
-        if h == 0:
-            hs = list(range(1, half))
-            for i, (iq, beta) in zip(hs, factor(None, p_s, b_s, rl_s, hs, False, pr_s)):
-                iq_s[i] = iq
-                beta_s[i] = beta
         behind_own(h < last)
         if h < last:
             c = remote(tr_s, tr_r.at[h], tr_ss.at[h], tr_rs.at[h], x_peer)
             c.start()
             tails.append(c)
         if h == 0:
+            hs = list(range(1, half))
+            for i, (iq, beta) in zip(hs, factor(None, p_s, b_s, rl_s, hs, False, pr_s)):
+                iq_s[i] = iq
+                beta_s[i] = beta
             for i in hs:
                 send_betas(i)
         if h == EDGE_AT:

time: 17.2 us -> 17.2 us (level)
  no operation moved by 1% of the time
where the time goes in v6:
time: 17.2 us; the launch traced here: 17 us
  Pallas kernels  16.3 us (95%)
  local copies, waits for them, and re-layouts  0.71 us (4%)
    pallas_call x1, Pallas kernels, on_device(): pl.pallas_call(functools.partial(kernel, ny_parts, half), out_shape=pltpu...  16.3 us
    unnamed x1, local copies, waits for them, and re-layouts  0.71 us

profile of v6, /device:TPU:98, one launch (start us, length us, event | category | flops | bytes accessed | tf_op | source)
XLA Modules:
  0.0 17.0 jit_solution(6859396631229794284)
XLA Ops:
  0.0 16.3 %shard_map.64 = f32[64,8,128]{2,1,0:T(8,128)S(1)} custom-call(f32[64,8,128]{2,1,0:T(8,128)} %u_in.1, f32[64,8,128]{2,1,0:T(8,128)} %pc_in.1, f32[64,8,128]{2,1,0:T(8,128)} %lc_in.1, f32[64,8,128]{2,1,0:T(8,128)} %src_in.1, f32[8]{0:T(128)} %table.1, s32[4]{0:T(128)} %index.1), custom_call_target="tpu_custom_call" | custom-call | tf_op jit(solution)/shard_map/pallas_call | solution.py:576
  16.3 0.7 %copy.8 = f32[64,8,128]{2,1,0:T(8,128)} copy(f32[64,8,128]{2,1,0:T(8,128)S(1)} %shard_map.64) | data formatting | bytes 524288
